TPU v7x, 16 devices: a 4x2x1 block of a 4x4x8 slice. The times are simulated.
16 devices in a mesh: seqs: 2 (over y, z), states: 8 (over x, core).
Axes of the slice: x: 4, y: 2, z: 1, core: 2. Of those that a mesh axis runs over, the one named last changes fastest.
The devices are a block of a 4x4x8 slice.
Arguments:
- trans_mat: bfloat16 [16384, 16384], P(None, 'states')
- emit_mat: bfloat16 [16384, 10000], P('states')
- init_prob: float32 [16384], P('states')
- tokens: int32 [256, 32], P('seqs'), parts along dimension 0
Outputs:
- output 1: float32 [256, 32], P('seqs'), parts along dimension 0
- output 2: float32 [256, 16384], P('seqs', 'states'), parts along dimension 0
There are 2 independent parts. A program takes and returns all parts, laid end to end along the dimension named above; an argument that names none is the same for every part.
All inputs are finite; a program needn't handle non-finite values.
Results may differ from a plain program's by a relative error of at most 0.00272.
Values are sent between devices in bfloat16 or wider.
A program may use at most 768 MiB of HBM per device.

v0:
```python
import jax
import jax.numpy as jnp
from jax import lax
from jax.sharding import PartitionSpec as P


def solution(mesh):
    def local_forward(trans_mat, emit_mat, init_prob, tokens):
        k_total = trans_mat.shape[0]
        vocab_size = emit_mat.shape[1]
        emit_steps = jnp.transpose(jnp.take(emit_mat, tokens.T, axis=1), (1, 2, 0))
        first_h = init_prob[None, :] * emit_steps[0]
        row_total = lax.psum(jnp.sum(first_h, axis=-1), "states")
        alpha_start = first_h * (k_total / row_total)[:, None]

        def advance(alpha_prev, emit_t):
            alpha_all = lax.all_gather(alpha_prev.astype(jnp.bfloat16), "states", axis=1, tiled=True)
            mixed_u = jnp.dot(alpha_all, trans_mat, preferred_element_type=jnp.float32)
            raw_h = mixed_u * emit_t
            norm_c = lax.psum(jnp.sum(raw_h, axis=-1), "states") / k_total
            return raw_h / norm_c[:, None], jnp.log(norm_c * vocab_size)

        alpha_final, step_logs = lax.scan(advance, alpha_start, emit_steps[1:])
        step_loglik = jnp.concatenate([jnp.log(row_total * vocab_size)[:, None], step_logs.T], axis=1)
        return step_loglik, alpha_final

    return jax.shard_map(
        local_forward,
        mesh=mesh,
        in_specs=(P(None, "states"), P("states", None), P("states"), P("seqs", None)),
        out_specs=(P("seqs", None), P("seqs", "states")),
        check_vma=False,
    )
```

profile of v0, /device:TPU:113, one launch (start us, length us, event | category | flops | bytes accessed | tf_op | source)
XLA Modules:
  0.0 2260.3 jit_solution(17711232716936489875)
XLA Ops:
  7.9 95.9 %gather_fusion = bf16[4096,2048]{1,0:T(8,128)(2,1)} fusion(bf16[2048,10000]{0,1:T(8,128)(2,1)} %param.7, s32[4096]{0:T(1024)S(1)} %bitcast_clamp_fusion), kind=kCustom, calls=%fused_computation | custom fusion | bytes 33570816 | tf_op jit(solution)/shard_map/jit(_take)/gather | solution.py:11
  146.8 2105.7 %while.14 = (s32[]{:T(128)}, f32[128,2048]{1,0:T(8,128)S(1)}, f32[31,128]{1,0:T(8,128)S(1)}, bf16[16384,2048]{1,0:T(8,128)(2,1)}, bf16[31,128,2048]{2,1,0:T(8,128)(2,1)}, /*index=5*/s32[]{:T(128)}, s32[]{:T(128)}) while((s32[]{:T(128)}, f32[128,2048]{1,0:T(8,128)S(1)}, f32[31,128]{1,0:T(8,128)S(1)}, bf16[16384,2048]{1,0:T(8,128)(2,1)}, ...), condition=%wide.region_5.6_spmd, body=%wide.region_2.0_spmd.sunk | while | flops 8591245312 | bytes 90706560 | solution.py:23
  147.7 31.9 %all-gather.2.cloned.1.call-done = bf16[128,16384]{1,0:T(8,128)(2,1)} async-done(((bf16[128,2048]{1,0:T(8,128)(2,1)}), bf16[128,16384]{1,0:T(8,128)(2,1)}) %all-gather.2.cloned.1.call-update) | async-done | bytes 4194320 | tf_op jit(solution)/shard_map/while/body/eval_jaxpr/all_gather | solution.py:17
  179.6 25.1 %fusion.10 = (f32[128]{0:T(128)S(1)}, f32[128,2048]{1,0:T(8,128)S(1)}) fusion(bf16[31,128,2048]{2,1,0:T(8,128)(2,1)} %get-tuple-element.143, s32[]{:T(128)S(6)} %copy.10, bf16[128,16384]{1,0:T(8,128)(2,1)} %all-gather.2.cloned.1.call-done, bf16[16384,2048]{1,0:T(8,128)(2,1)} %get-tuple-element.142), kind=kOutput, calls=%fused_computation.16.clone.1 | convolution fusion | flops 8590721024 | bytes 72876544 | tf_op jit(solution)/shard_map/while/body/eval_jaxpr/dot_general | solution.py:18
  218.0 29.6 %all-gather.2.cloned.1.call-done = bf16[128,16384]{1,0:T(8,128)(2,1)} async-done(((bf16[128,2048]{1,0:T(8,128)(2,1)}), bf16[128,16384]{1,0:T(8,128)(2,1)}) %all-gather.2.cloned.1.call-update) | async-done | bytes 4194320 | tf_op jit(solution)/shard_map/while/body/eval_jaxpr/all_gather | solution.py:17
  247.6 25.1 %fusion.10 = (f32[128]{0:T(128)S(1)}, f32[128,2048]{1,0:T(8,128)S(1)}) fusion(bf16[31,128,2048]{2,1,0:T(8,128)(2,1)} %get-tuple-element.143, s32[]{:T(128)S(6)} %copy.10, bf16[128,16384]{1,0:T(8,128)(2,1)} %all-gather.2.cloned.1.call-done, bf16[16384,2048]{1,0:T(8,128)(2,1)} %get-tuple-element.142), kind=kOutput, calls=%fused_computation.16.clone.1 | convolution fusion | flops 8590721024 | bytes 72876544 | tf_op jit(solution)/shard_map/while/body/eval_jaxpr/dot_general | solution.py:18
  286.0 29.6 %all-gather.2.cloned.1.call-done = bf16[128,16384]{1,0:T(8,128)(2,1)} async-done(((bf16[128,2048]{1,0:T(8,128)(2,1)}), bf16[128,16384]{1,0:T(8,128)(2,1)}) %all-gather.2.cloned.1.call-update) | async-done | bytes 4194320 | tf_op jit(solution)/shard_map/while/body/eval_jaxpr/all_gather | solution.py:17
  315.6 25.1 %fusion.10 = (f32[128]{0:T(128)S(1)}, f32[128,2048]{1,0:T(8,128)S(1)}) fusion(bf16[31,128,2048]{2,1,0:T(8,128)(2,1)} %get-tuple-element.143, s32[]{:T(128)S(6)} %copy.10, bf16[128,16384]{1,0:T(8,128)(2,1)} %all-gather.2.cloned.1.call-done, bf16[16384,2048]{1,0:T(8,128)(2,1)} %get-tuple-element.142), kind=kOutput, calls=%fused_computation.16.clone.1 | convolution fusion | flops 8590721024 | bytes 72876544 | tf_op jit(solution)/shard_map/while/body/eval_jaxpr/dot_general | solution.py:18
  354.0 29.3 %all-gather.2.cloned.1.call-done = bf16[128,16384]{1,0:T(8,128)(2,1)} async-done(((bf16[128,2048]{1,0:T(8,128)(2,1)}), bf16[128,16384]{1,0:T(8,128)(2,1)}) %all-gather.2.cloned.1.call-update) | async-done | bytes 4194320 | tf_op jit(solution)/shard_map/while/body/eval_jaxpr/all_gather | solution.py:17
  421.7 29.3 %all-gather.2.cloned.1.call-done = bf16[128,16384]{1,0:T(8,128)(2,1)} async-done(((bf16[128,2048]{1,0:T(8,128)(2,1)}), bf16[128,16384]{1,0:T(8,128)(2,1)}) %all-gather.2.cloned.1.call-update) | async-done | bytes 4194320 | tf_op jit(solution)/shard_map/while/body/eval_jaxpr/all_gather | solution.py:17
  451.0 25.1 %fusion.10 = (f32[128]{0:T(128)S(1)}, f32[128,2048]{1,0:T(8,128)S(1)}) fusion(bf16[31,128,2048]{2,1,0:T(8,128)(2,1)} %get-tuple-element.143, s32[]{:T(128)S(6)} %copy.10, bf16[128,16384]{1,0:T(8,128)(2,1)} %all-gather.2.cloned.1.call-done, bf16[16384,2048]{1,0:T(8,128)(2,1)} %get-tuple-element.142), kind=kOutput, calls=%fused_computation.16.clone.1 | convolution fusion | flops 8590721024 | bytes 72876544 | tf_op jit(solution)/shard_map/while/body/eval_jaxpr/dot_general | solution.py:18
  489.4 29.3 %all-gather.2.cloned.1.call-done = bf16[128,16384]{1,0:T(8,128)(2,1)} async-done(((bf16[128,2048]{1,0:T(8,128)(2,1)}), bf16[128,16384]{1,0:T(8,128)(2,1)}) %all-gather.2.cloned.1.call-update) | async-done | bytes 4194320 | tf_op jit(solution)/shard_map/while/body/eval_jaxpr/all_gather | solution.py:17
  557.1 29.6 %all-gather.2.cloned.1.call-done = bf16[128,16384]{1,0:T(8,128)(2,1)} async-done(((bf16[128,2048]{1,0:T(8,128)(2,1)}), bf16[128,16384]{1,0:T(8,128)(2,1)}) %all-gather.2.cloned.1.call-update) | async-done | bytes 4194320 | tf_op jit(solution)/shard_map/while/body/eval_jaxpr/all_gather | solution.py:17
  586.7 25.1 %fusion.10 = (f32[128]{0:T(128)S(1)}, f32[128,2048]{1,0:T(8,128)S(1)}) fusion(bf16[31,128,2048]{2,1,0:T(8,128)(2,1)} %get-tuple-element.143, s32[]{:T(128)S(6)} %copy.10, bf16[128,16384]{1,0:T(8,128)(2,1)} %all-gather.2.cloned.1.call-done, bf16[16384,2048]{1,0:T(8,128)(2,1)} %get-tuple-element.142), kind=kOutput, calls=%fused_computation.16.clone.1 | convolution fusion | flops 8590721024 | bytes 72876544 | tf_op jit(solution)/shard_map/while/body/eval_jaxpr/dot_general | solution.py:18
  625.1 29.6 %all-gather.2.cloned.1.call-done = bf16[128,16384]{1,0:T(8,128)(2,1)} async-done(((bf16[128,2048]{1,0:T(8,128)(2,1)}), bf16[128,16384]{1,0:T(8,128)(2,1)}) %all-gather.2.cloned.1.call-update) | async-done | bytes 4194320 | tf_op jit(solution)/shard_map/while/body/eval_jaxpr/all_gather | solution.py:17
  654.7 25.1 %fusion.10 = (f32[128]{0:T(128)S(1)}, f32[128,2048]{1,0:T(8,128)S(1)}) fusion(bf16[31,128,2048]{2,1,0:T(8,128)(2,1)} %get-tuple-element.143, s32[]{:T(128)S(6)} %copy.10, bf16[128,16384]{1,0:T(8,128)(2,1)} %all-gather.2.cloned.1.call-done, bf16[16384,2048]{1,0:T(8,128)(2,1)} %get-tuple-element.142), kind=kOutput, calls=%fused_computation.16.clone.1 | convolution fusion | flops 8590721024 | bytes 72876544 | tf_op jit(solution)/shard_map/while/body/eval_jaxpr/dot_general | solution.py:18
  693.1 29.6 %all-gather.2.cloned.1.call-done = bf16[128,16384]{1,0:T(8,128)(2,1)} async-done(((bf16[128,2048]{1,0:T(8,128)(2,1)}), bf16[128,16384]{1,0:T(8,128)(2,1)}) %all-gather.2.cloned.1.call-update) | async-done | bytes 4194320 | tf_op jit(solution)/shard_map/while/body/eval_jaxpr/all_gather | solution.py:17
  722.7 25.1 %fusion.10 = (f32[128]{0:T(128)S(1)}, f32[128,2048]{1,0:T(8,128)S(1)}) fusion(bf16[31,128,2048]{2,1,0:T(8,128)(2,1)} %get-tuple-element.143, s32[]{:T(128)S(6)} %copy.10, bf16[128,16384]{1,0:T(8,128)(2,1)} %all-gather.2.cloned.1.call-done, bf16[16384,2048]{1,0:T(8,128)(2,1)} %get-tuple-element.142), kind=kOutput, calls=%fused_computation.16.clone.1 | convolution fusion | flops 8590721024 | bytes 72876544 | tf_op jit(solution)/shard_map/while/body/eval_jaxpr/dot_general | solution.py:18
  761.1 29.3 %all-gather.2.cloned.1.call-done = bf16[128,16384]{1,0:T(8,128)(2,1)} async-done(((bf16[128,2048]{1,0:T(8,128)(2,1)}), bf16[128,16384]{1,0:T(8,128)(2,1)}) %all-gather.2.cloned.1.call-update) | async-done | bytes 4194320 | tf_op jit(solution)/shard_map/while/body/eval_jaxpr/all_gather | solution.py:17
  790.4 25.1 %fusion.10 = (f32[128]{0:T(128)S(1)}, f32[128,2048]{1,0:T(8,128)S(1)}) fusion(bf16[31,128,2048]{2,1,0:T(8,128)(2,1)} %get-tuple-element.143, s32[]{:T(128)S(6)} %copy.10, bf16[128,16384]{1,0:T(8,128)(2,1)} %all-gather.2.cloned.1.call-done, bf16[16384,2048]{1,0:T(8,128)(2,1)} %get-tuple-element.142), kind=kOutput, calls=%fused_computation.16.clone.1 | convolution fusion | flops 8590721024 | bytes 72876544 | tf_op jit(solution)/shard_map/while/body/eval_jaxpr/dot_general | solution.py:18
  828.8 29.6 %all-gather.2.cloned.1.call-done = bf16[128,16384]{1,0:T(8,128)(2,1)} async-done(((bf16[128,2048]{1,0:T(8,128)(2,1)}), bf16[128,16384]{1,0:T(8,128)(2,1)}) %all-gather.2.cloned.1.call-update) | async-done | bytes 4194320 | tf_op jit(solution)/shard_map/while/body/eval_jaxpr/all_gather | solution.py:17
  858.4 25.1 %fusion.10 = (f32[128]{0:T(128)S(1)}, f32[128,2048]{1,0:T(8,128)S(1)}) fusion(bf16[31,128,2048]{2,1,0:T(8,128)(2,1)} %get-tuple-element.143, s32[]{:T(128)S(6)} %copy.10, bf16[128,16384]{1,0:T(8,128)(2,1)} %all-gather.2.cloned.1.call-done, bf16[16384,2048]{1,0:T(8,128)(2,1)} %get-tuple-element.142), kind=kOutput, calls=%fused_computation.16.clone.1 | convolution fusion | flops 8590721024 | bytes 72876544 | tf_op jit(solution)/shard_map/while/body/eval_jaxpr/dot_general | solution.py:18
  896.8 29.3 %all-gather.2.cloned.1.call-done = bf16[128,16384]{1,0:T(8,128)(2,1)} async-done(((bf16[128,2048]{1,0:T(8,128)(2,1)}), bf16[128,16384]{1,0:T(8,128)(2,1)}) %all-gather.2.cloned.1.call-update) | async-done | bytes 4194320 | tf_op jit(solution)/shard_map/while/body/eval_jaxpr/all_gather | solution.py:17
  964.5 29.6 %all-gather.2.cloned.1.call-done = bf16[128,16384]{1,0:T(8,128)(2,1)} async-done(((bf16[128,2048]{1,0:T(8,128)(2,1)}), bf16[128,16384]{1,0:T(8,128)(2,1)}) %all-gather.2.cloned.1.call-update) | async-done | bytes 4194320 | tf_op jit(solution)/shard_map/while/body/eval_jaxpr/all_gather | solution.py:17
  994.1 25.1 %fusion.10 = (f32[128]{0:T(128)S(1)}, f32[128,2048]{1,0:T(8,128)S(1)}) fusion(bf16[31,128,2048]{2,1,0:T(8,128)(2,1)} %get-tuple-element.143, s32[]{:T(128)S(6)} %copy.10, bf16[128,16384]{1,0:T(8,128)(2,1)} %all-gather.2.cloned.1.call-done, bf16[16384,2048]{1,0:T(8,128)(2,1)} %get-tuple-element.142), kind=kOutput, calls=%fused_computation.16.clone.1 | convolution fusion | flops 8590721024 | bytes 72876544 | tf_op jit(solution)/shard_map/while/body/eval_jaxpr/dot_general | solution.py:18
  1032.5 29.3 %all-gather.2.cloned.1.call-done = bf16[128,16384]{1,0:T(8,128)(2,1)} async-done(((bf16[128,2048]{1,0:T(8,128)(2,1)}), bf16[128,16384]{1,0:T(8,128)(2,1)}) %all-gather.2.cloned.1.call-update) | async-done | bytes 4194320 | tf_op jit(solution)/shard_map/while/body/eval_jaxpr/all_gather | solution.py:17
  1100.2 29.3 %all-gather.2.cloned.1.call-done = bf16[128,16384]{1,0:T(8,128)(2,1)} async-done(((bf16[128,2048]{1,0:T(8,128)(2,1)}), bf16[128,16384]{1,0:T(8,128)(2,1)}) %all-gather.2.cloned.1.call-update) | async-done | bytes 4194320 | tf_op jit(solution)/shard_map/while/body/eval_jaxpr/all_gather | solution.py:17
  1129.5 25.1 %fusion.10 = (f32[128]{0:T(128)S(1)}, f32[128,2048]{1,0:T(8,128)S(1)}) fusion(bf16[31,128,2048]{2,1,0:T(8,128)(2,1)} %get-tuple-element.143, s32[]{:T(128)S(6)} %copy.10, bf16[128,16384]{1,0:T(8,128)(2,1)} %all-gather.2.cloned.1.call-done, bf16[16384,2048]{1,0:T(8,128)(2,1)} %get-tuple-element.142), kind=kOutput, calls=%fused_computation.16.clone.1 | convolution fusion | flops 8590721024 | bytes 72876544 | tf_op jit(solution)/shard_map/while/body/eval_jaxpr/dot_general | solution.py:18
  1167.9 29.3 %all-gather.2.cloned.1.call-done = bf16[128,16384]{1,0:T(8,128)(2,1)} async-done(((bf16[128,2048]{1,0:T(8,128)(2,1)}), bf16[128,16384]{1,0:T(8,128)(2,1)}) %all-gather.2.cloned.1.call-update) | async-done | bytes 4194320 | tf_op jit(solution)/shard_map/while/body/eval_jaxpr/all_gather | solution.py:17
  1235.6 29.3 %all-gather.2.cloned.1.call-done = bf16[128,16384]{1,0:T(8,128)(2,1)} async-done(((bf16[128,2048]{1,0:T(8,128)(2,1)}), bf16[128,16384]{1,0:T(8,128)(2,1)}) %all-gather.2.cloned.1.call-update) | async-done | bytes 4194320 | tf_op jit(solution)/shard_map/while/body/eval_jaxpr/all_gather | solution.py:17
  1264.9 25.1 %fusion.10 = (f32[128]{0:T(128)S(1)}, f32[128,2048]{1,0:T(8,128)S(1)}) fusion(bf16[31,128,2048]{2,1,0:T(8,128)(2,1)} %get-tuple-element.143, s32[]{:T(128)S(6)} %copy.10, bf16[128,16384]{1,0:T(8,128)(2,1)} %all-gather.2.cloned.1.call-done, bf16[16384,2048]{1,0:T(8,128)(2,1)} %get-tuple-element.142), kind=kOutput, calls=%fused_computation.16.clone.1 | convolution fusion | flops 8590721024 | bytes 72876544 | tf_op jit(solution)/shard_map/while/body/eval_jaxpr/dot_general | solution.py:18
  1303.3 29.3 %all-gather.2.cloned.1.call-done = bf16[128,16384]{1,0:T(8,128)(2,1)} async-done(((bf16[128,2048]{1,0:T(8,128)(2,1)}), bf16[128,16384]{1,0:T(8,128)(2,1)}) %all-gather.2.cloned.1.call-update) | async-done | bytes 4194320 | tf_op jit(solution)/shard_map/while/body/eval_jaxpr/all_gather | solution.py:17
  1332.6 25.1 %fusion.10 = (f32[128]{0:T(128)S(1)}, f32[128,2048]{1,0:T(8,128)S(1)}) fusion(bf16[31,128,2048]{2,1,0:T(8,128)(2,1)} %get-tuple-element.143, s32[]{:T(128)S(6)} %copy.10, bf16[128,16384]{1,0:T(8,128)(2,1)} %all-gather.2.cloned.1.call-done, bf16[16384,2048]{1,0:T(8,128)(2,1)} %get-tuple-element.142), kind=kOutput, calls=%fused_computation.16.clone.1 | convolution fusion | flops 8590721024 | bytes 72876544 | tf_op jit(solution)/shard_map/while/body/eval_jaxpr/dot_general | solution.py:18
  1371.0 29.6 %all-gather.2.cloned.1.call-done = bf16[128,16384]{1,0:T(8,128)(2,1)} async-done(((bf16[128,2048]{1,0:T(8,128)(2,1)}), bf16[128,16384]{1,0:T(8,128)(2,1)}) %all-gather.2.cloned.1.call-update) | async-done | bytes 4194320 | tf_op jit(solution)/shard_map/while/body/eval_jaxpr/all_gather | solution.py:17
  1400.6 25.1 %fusion.10 = (f32[128]{0:T(128)S(1)}, f32[128,2048]{1,0:T(8,128)S(1)}) fusion(bf16[31,128,2048]{2,1,0:T(8,128)(2,1)} %get-tuple-element.143, s32[]{:T(128)S(6)} %copy.10, bf16[128,16384]{1,0:T(8,128)(2,1)} %all-gather.2.cloned.1.call-done, bf16[16384,2048]{1,0:T(8,128)(2,1)} %get-tuple-element.142), kind=kOutput, calls=%fused_computation.16.clone.1 | convolution fusion | flops 8590721024 | bytes 72876544 | tf_op jit(solution)/shard_map/while/body/eval_jaxpr/dot_general | solution.py:18
  1439.0 29.3 %all-gather.2.cloned.1.call-done = bf16[128,16384]{1,0:T(8,128)(2,1)} async-done(((bf16[128,2048]{1,0:T(8,128)(2,1)}), bf16[128,16384]{1,0:T(8,128)(2,1)}) %all-gather.2.cloned.1.call-update) | async-done | bytes 4194320 | tf_op jit(solution)/shard_map/while/body/eval_jaxpr/all_gather | solution.py:17
  1506.7 29.6 %all-gather.2.cloned.1.call-done = bf16[128,16384]{1,0:T(8,128)(2,1)} async-done(((bf16[128,2048]{1,0:T(8,128)(2,1)}), bf16[128,16384]{1,0:T(8,128)(2,1)}) %all-gather.2.cloned.1.call-update) | async-done | bytes 4194320 | tf_op jit(solution)/shard_map/while/body/eval_jaxpr/all_gather | solution.py:17
  1574.7 29.6 %all-gather.2.cloned.1.call-done = bf16[128,16384]{1,0:T(8,128)(2,1)} async-done(((bf16[128,2048]{1,0:T(8,128)(2,1)}), bf16[128,16384]{1,0:T(8,128)(2,1)}) %all-gather.2.cloned.1.call-update) | async-done | bytes 4194320 | tf_op jit(solution)/shard_map/while/body/eval_jaxpr/all_gather | solution.py:17
  1642.7 29.6 %all-gather.2.cloned.1.call-done = bf16[128,16384]{1,0:T(8,128)(2,1)} async-done(((bf16[128,2048]{1,0:T(8,128)(2,1)}), bf16[128,16384]{1,0:T(8,128)(2,1)}) %all-gather.2.cloned.1.call-update) | async-done | bytes 4194320 | tf_op jit(solution)/shard_map/while/body/eval_jaxpr/all_gather | solution.py:17
  1710.7 29.3 %all-gather.2.cloned.1.call-done = bf16[128,16384]{1,0:T(8,128)(2,1)} async-done(((bf16[128,2048]{1,0:T(8,128)(2,1)}), bf16[128,16384]{1,0:T(8,128)(2,1)}) %all-gather.2.cloned.1.call-update) | async-done | bytes 4194320 | tf_op jit(solution)/shard_map/while/body/eval_jaxpr/all_gather | solution.py:17
  1778.4 29.6 %all-gather.2.cloned.1.call-done = bf16[128,16384]{1,0:T(8,128)(2,1)} async-done(((bf16[128,2048]{1,0:T(8,128)(2,1)}), bf16[128,16384]{1,0:T(8,128)(2,1)}) %all-gather.2.cloned.1.call-update) | async-done | bytes 4194320 | tf_op jit(solution)/shard_map/while/body/eval_jaxpr/all_gather | solution.py:17
  1808.0 25.1 %fusion.10 = (f32[128]{0:T(128)S(1)}, f32[128,2048]{1,0:T(8,128)S(1)}) fusion(bf16[31,128,2048]{2,1,0:T(8,128)(2,1)} %get-tuple-element.143, s32[]{:T(128)S(6)} %copy.10, bf16[128,16384]{1,0:T(8,128)(2,1)} %all-gather.2.cloned.1.call-done, bf16[16384,2048]{1,0:T(8,128)(2,1)} %get-tuple-element.142), kind=kOutput, calls=%fused_computation.16.clone.1 | convolution fusion | flops 8590721024 | bytes 72876544 | tf_op jit(solution)/shard_map/while/body/eval_jaxpr/dot_general | solution.py:18
  1846.4 29.3 %all-gather.2.cloned.1.call-done = bf16[128,16384]{1,0:T(8,128)(2,1)} async-done(((bf16[128,2048]{1,0:T(8,128)(2,1)}), bf16[128,16384]{1,0:T(8,128)(2,1)}) %all-gather.2.cloned.1.call-update) | async-done | bytes 4194320 | tf_op jit(solution)/shard_map/while/body/eval_jaxpr/all_gather | solution.py:17
  1914.1 29.3 %all-gather.2.cloned.1.call-done = bf16[128,16384]{1,0:T(8,128)(2,1)} async-done(((bf16[128,2048]{1,0:T(8,128)(2,1)}), bf16[128,16384]{1,0:T(8,128)(2,1)}) %all-gather.2.cloned.1.call-update) | async-done | bytes 4194320 | tf_op jit(solution)/shard_map/while/body/eval_jaxpr/all_gather | solution.py:17
  1981.8 29.6 %all-gather.2.cloned.1.call-done = bf16[128,16384]{1,0:T(8,128)(2,1)} async-done(((bf16[128,2048]{1,0:T(8,128)(2,1)}), bf16[128,16384]{1,0:T(8,128)(2,1)}) %all-gather.2.cloned.1.call-update) | async-done | bytes 4194320 | tf_op jit(solution)/shard_map/while/body/eval_jaxpr/all_gather | solution.py:17
  2049.8 29.6 %all-gather.2.cloned.1.call-done = bf16[128,16384]{1,0:T(8,128)(2,1)} async-done(((bf16[128,2048]{1,0:T(8,128)(2,1)}), bf16[128,16384]{1,0:T(8,128)(2,1)}) %all-gather.2.cloned.1.call-update) | async-done | bytes 4194320 | tf_op jit(solution)/shard_map/while/body/eval_jaxpr/all_gather | solution.py:17
  2117.8 29.3 %all-gather.2.cloned.1.call-done = bf16[128,16384]{1,0:T(8,128)(2,1)} async-done(((bf16[128,2048]{1,0:T(8,128)(2,1)}), bf16[128,16384]{1,0:T(8,128)(2,1)}) %all-gather.2.cloned.1.call-update) | async-done | bytes 4194320 | tf_op jit(solution)/shard_map/while/body/eval_jaxpr/all_gather | solution.py:17
  2185.5 29.6 %all-gather.2.cloned.1.call-done = bf16[128,16384]{1,0:T(8,128)(2,1)} async-done(((bf16[128,2048]{1,0:T(8,128)(2,1)}), bf16[128,16384]{1,0:T(8,128)(2,1)}) %all-gather.2.cloned.1.call-update) | async-done | bytes 4194320 | tf_op jit(solution)/shard_map/while/body/eval_jaxpr/all_gather | solution.py:17
  (251 shorter events, 857.2 us)
Async XLA Ops:
  7.9 95.9 %copy-start.2 = (s32[128,32]{0,1:T(8,128)S(1)}, s32[128,32]{0,1:T(8,128)}, u32[]{:S(2)}) copy-start(s32[128,32]{0,1:T(8,128)} %param.9) | copy-start | bytes 49156
  103.8 14.2 copy-start.3
  112.3 5.7 copy-start
  146.8 32.9 %all-gather.2.cloned.1.call-start = ((), (), s32[]{:S(2)}) async-start(), calls=%async_computation | async-start | bytes 4718592 | tf_op jit(solution)/shard_map/while/body/eval_jaxpr/all_gather | solution.py:17
  217.0 30.6 %all-gather.2.cloned.1.call-start = ((), (), s32[]{:S(2)}) async-start(), calls=%async_computation | async-start | bytes 4718592 | tf_op jit(solution)/shard_map/while/body/eval_jaxpr/all_gather | solution.py:17
  285.0 30.6 %all-gather.2.cloned.1.call-start = ((), (), s32[]{:S(2)}) async-start(), calls=%async_computation | async-start | bytes 4718592 | tf_op jit(solution)/shard_map/while/body/eval_jaxpr/all_gather | solution.py:17
  353.0 30.3 %all-gather.2.cloned.1.call-start = ((), (), s32[]{:S(2)}) async-start(), calls=%async_computation | async-start | bytes 4718592 | tf_op jit(solution)/shard_map/while/body/eval_jaxpr/all_gather | solution.py:17
  420.7 30.3 %all-gather.2.cloned.1.call-start = ((), (), s32[]{:S(2)}) async-start(), calls=%async_computation | async-start | bytes 4718592 | tf_op jit(solution)/shard_map/while/body/eval_jaxpr/all_gather | solution.py:17
  488.4 30.3 %all-gather.2.cloned.1.call-start = ((), (), s32[]{:S(2)}) async-start(), calls=%async_computation | async-start | bytes 4718592 | tf_op jit(solution)/shard_map/while/body/eval_jaxpr/all_gather | solution.py:17
  556.1 30.6 %all-gather.2.cloned.1.call-start = ((), (), s32[]{:S(2)}) async-start(), calls=%async_computation | async-start | bytes 4718592 | tf_op jit(solution)/shard_map/while/body/eval_jaxpr/all_gather | solution.py:17
  624.1 30.6 %all-gather.2.cloned.1.call-start = ((), (), s32[]{:S(2)}) async-start(), calls=%async_computation | async-start | bytes 4718592 | tf_op jit(solution)/shard_map/while/body/eval_jaxpr/all_gather | solution.py:17
  692.1 30.6 %all-gather.2.cloned.1.call-start = ((), (), s32[]{:S(2)}) async-start(), calls=%async_computation | async-start | bytes 4718592 | tf_op jit(solution)/shard_map/while/body/eval_jaxpr/all_gather | solution.py:17
  760.1 30.3 %all-gather.2.cloned.1.call-start = ((), (), s32[]{:S(2)}) async-start(), calls=%async_computation | async-start | bytes 4718592 | tf_op jit(solution)/shard_map/while/body/eval_jaxpr/all_gather | solution.py:17
  827.8 30.6 %all-gather.2.cloned.1.call-start = ((), (), s32[]{:S(2)}) async-start(), calls=%async_computation | async-start | bytes 4718592 | tf_op jit(solution)/shard_map/while/body/eval_jaxpr/all_gather | solution.py:17
  895.8 30.3 %all-gather.2.cloned.1.call-start = ((), (), s32[]{:S(2)}) async-start(), calls=%async_computation | async-start | bytes 4718592 | tf_op jit(solution)/shard_map/while/body/eval_jaxpr/all_gather | solution.py:17
  963.5 30.6 %all-gather.2.cloned.1.call-start = ((), (), s32[]{:S(2)}) async-start(), calls=%async_computation | async-start | bytes 4718592 | tf_op jit(solution)/shard_map/while/body/eval_jaxpr/all_gather | solution.py:17
  1031.5 30.3 %all-gather.2.cloned.1.call-start = ((), (), s32[]{:S(2)}) async-start(), calls=%async_computation | async-start | bytes 4718592 | tf_op jit(solution)/shard_map/while/body/eval_jaxpr/all_gather | solution.py:17
  1099.2 30.3 %all-gather.2.cloned.1.call-start = ((), (), s32[]{:S(2)}) async-start(), calls=%async_computation | async-start | bytes 4718592 | tf_op jit(solution)/shard_map/while/body/eval_jaxpr/all_gather | solution.py:17
  1166.9 30.3 %all-gather.2.cloned.1.call-start = ((), (), s32[]{:S(2)}) async-start(), calls=%async_computation | async-start | bytes 4718592 | tf_op jit(solution)/shard_map/while/body/eval_jaxpr/all_gather | solution.py:17
  1234.6 30.3 %all-gather.2.cloned.1.call-start = ((), (), s32[]{:S(2)}) async-start(), calls=%async_computation | async-start | bytes 4718592 | tf_op jit(solution)/shard_map/while/body/eval_jaxpr/all_gather | solution.py:17
  1302.3 30.3 %all-gather.2.cloned.1.call-start = ((), (), s32[]{:S(2)}) async-start(), calls=%async_computation | async-start | bytes 4718592 | tf_op jit(solution)/shard_map/while/body/eval_jaxpr/all_gather | solution.py:17
  1370.0 30.6 %all-gather.2.cloned.1.call-start = ((), (), s32[]{:S(2)}) async-start(), calls=%async_computation | async-start | bytes 4718592 | tf_op jit(solution)/shard_map/while/body/eval_jaxpr/all_gather | solution.py:17
  1438.0 30.3 %all-gather.2.cloned.1.call-start = ((), (), s32[]{:S(2)}) async-start(), calls=%async_computation | async-start | bytes 4718592 | tf_op jit(solution)/shard_map/while/body/eval_jaxpr/all_gather | solution.py:17
  1505.7 30.6 %all-gather.2.cloned.1.call-start = ((), (), s32[]{:S(2)}) async-start(), calls=%async_computation | async-start | bytes 4718592 | tf_op jit(solution)/shard_map/while/body/eval_jaxpr/all_gather | solution.py:17
  1573.7 30.6 %all-gather.2.cloned.1.call-start = ((), (), s32[]{:S(2)}) async-start(), calls=%async_computation | async-start | bytes 4718592 | tf_op jit(solution)/shard_map/while/body/eval_jaxpr/all_gather | solution.py:17
  1641.7 30.6 %all-gather.2.cloned.1.call-start = ((), (), s32[]{:S(2)}) async-start(), calls=%async_computation | async-start | bytes 4718592 | tf_op jit(solution)/shard_map/while/body/eval_jaxpr/all_gather | solution.py:17
  1709.7 30.3 %all-gather.2.cloned.1.call-start = ((), (), s32[]{:S(2)}) async-start(), calls=%async_computation | async-start | bytes 4718592 | tf_op jit(solution)/shard_map/while/body/eval_jaxpr/all_gather | solution.py:17
  1777.4 30.6 %all-gather.2.cloned.1.call-start = ((), (), s32[]{:S(2)}) async-start(), calls=%async_computation | async-start | bytes 4718592 | tf_op jit(solution)/shard_map/while/body/eval_jaxpr/all_gather | solution.py:17
  1845.4 30.3 %all-gather.2.cloned.1.call-start = ((), (), s32[]{:S(2)}) async-start(), calls=%async_computation | async-start | bytes 4718592 | tf_op jit(solution)/shard_map/while/body/eval_jaxpr/all_gather | solution.py:17
  1913.1 30.3 %all-gather.2.cloned.1.call-start = ((), (), s32[]{:S(2)}) async-start(), calls=%async_computation | async-start | bytes 4718592 | tf_op jit(solution)/shard_map/while/body/eval_jaxpr/all_gather | solution.py:17
  1980.8 30.6 %all-gather.2.cloned.1.call-start = ((), (), s32[]{:S(2)}) async-start(), calls=%async_computation | async-start | bytes 4718592 | tf_op jit(solution)/shard_map/while/body/eval_jaxpr/all_gather | solution.py:17
  2048.8 30.6 %all-gather.2.cloned.1.call-start = ((), (), s32[]{:S(2)}) async-start(), calls=%async_computation | async-start | bytes 4718592 | tf_op jit(solution)/shard_map/while/body/eval_jaxpr/all_gather | solution.py:17
  2116.8 30.3 %all-gather.2.cloned.1.call-start = ((), (), s32[]{:S(2)}) async-start(), calls=%async_computation | async-start | bytes 4718592 | tf_op jit(solution)/shard_map/while/body/eval_jaxpr/all_gather | solution.py:17
  2184.5 30.6 %all-gather.2.cloned.1.call-start = ((), (), s32[]{:S(2)}) async-start(), calls=%async_computation | async-start | bytes 4718592 | tf_op jit(solution)/shard_map/while/body/eval_jaxpr/all_gather | solution.py:17
  2252.5 1.0 copy-start.1
Sparse Core Ops, SparseCore 0:
  149.7 29.8 all-gather.1
  220.0 27.5 all-gather.1
  288.0 27.5 all-gather.1
  355.7 27.5 all-gather.1
  423.4 27.5 all-gather.1
  491.1 27.5 all-gather.1
  559.1 27.5 all-gather.1
  627.1 27.5 all-gather.1
  695.1 27.5 all-gather.1
  762.8 27.5 all-gather.1
  830.8 27.5 all-gather.1
  898.5 27.5 all-gather.1
  966.5 27.5 all-gather.1
  1034.2 27.5 all-gather.1
  1101.9 27.5 all-gather.1
  1169.6 27.5 all-gather.1
  1237.3 27.5 all-gather.1
  1305.0 27.5 all-gather.1
  1373.0 27.5 all-gather.1
  1440.7 27.5 all-gather.1
  1508.7 27.5 all-gather.1
  1576.7 27.5 all-gather.1
  1644.7 27.5 all-gather.1
  1712.4 27.5 all-gather.1
  1780.4 27.5 all-gather.1
  1848.1 27.5 all-gather.1
  1915.8 27.5 all-gather.1
  1983.8 27.5 all-gather.1
  2051.8 27.5 all-gather.1
  2119.5 27.5 all-gather.1
  2187.5 27.5 all-gather.1
where the time goes:
time: 2260 us
  waiting for transfers between devices  917 us (41%)
  matrix products  777 us (34%)
  blocking collectives  389 us (17%)
  local copies, waits for them, and re-layouts  117 us (5%)
  other arithmetic  43.1 us (2%)
    all_gather x31, waiting for transfers between devices, advance(): lax.all_gather(alpha_prev.astype(jnp.bfloat16), 'states', axis=1, tiled=T...  916 us
    dot_general x31, matrix products, advance(): mixed_u = jnp.dot(alpha_all, trans_mat, preferred_element_type=jnp.float32)  777 us
    psum x31, blocking collectives, advance(): norm_c = lax.psum(jnp.sum(raw_h, axis=-1), 'states') / k_total  375 us
    gather x1, local copies, waits for them, and re-layouts, local_forward(): emit_steps = jnp.transpose(jnp.take(emit_mat, tokens.T, axis=1), (1, 2, 0))  95.9 us
  transfers between devices with their start and end apart: 31, of which 31 were waited for; matrix products, arithmetic and copies ran while one was open for 0% of the time, Pallas kernels for 0%

commit v1 on v0

v1 whole, which is shorter than its diff:
```python
import functools

import jax
import jax.numpy as jnp
from jax import lax
from jax.experimental import pallas as pl
from jax.experimental.pallas import tpu as pltpu
from jax.sharding import PartitionSpec as P

MESH = pl.DeviceIdType.MESH
F32 = jnp.float32
BF16 = jnp.bfloat16
LANES = 128
SLOTS = 6
TILE = 256


def _when(cond, fn):
    if cond is True:
        fn()
    else:
        pl.when(cond)(fn)


def _forward_kernel(
    dims, a_hbm, e_hbm, pi_ref, tot_ref, out_ref,
    ad, ap, sb, go, gl, gd, gp, eb, cb, accv,
    a_sem, sb_sem, e_sem, own_s, pl_s, pl_r, d_r, f_s, dp_s, dp_r, c_s, c_r,
):
    n, steps, hb, kl = dims
    ck = kl // 4
    nx = n // 2
    k_total = n * kl
    ntiles = kl // TILE

    def run():
        me = lax.axis_index("states")
        x, core = me // 2, me % 2
        partner = 2 * x + 1 - core
        xr, xl, xf = (x + 1) % nx, (x + nx - 1) % nx, (x + 2) % nx
        right, left = 2 * xr + core, 2 * xl + core

        def remote(src, dst, ss, rs, dev):
            return pltpu.make_async_remote_copy(
                src_ref=src, dst_ref=dst, send_sem=ss, recv_sem=rs,
                device_id={"states": dev}, device_id_type=MESH,
            )

        def mm(half, parts):
            for nt in range(ntiles):
                cols = pl.ds(nt * TILE, TILE)
                total = accv[half, :, cols]
                for lhs, rhs in parts:
                    for q in range(rhs.shape[0]):
                        total += jnp.dot(lhs[q], rhs[q, :, cols], preferred_element_type=F32)
                accv[half, :, cols] = total

        def mm_joint(old, lhs, rhs, shared):
            for nt in range(ntiles):
                cols = pl.ds(nt * TILE, TILE)
                both = jnp.concatenate([accv[0, :, cols], accv[1, :, cols]], axis=0)
                for q in range(4):
                    rows = jnp.concatenate([shared[0, q], shared[1, q]], axis=0)
                    both += jnp.dot(rows, sb[q, :, cols], preferred_element_type=F32)
                own = both[old * hb : (old + 1) * hb]
                for q in range(rhs.shape[0]):
                    own += jnp.dot(lhs[q], rhs[q, :, cols], preferred_element_type=F32)
                accv[old, :, cols] = own
                accv[1 - old, :, cols] = both[(1 - old) * hb : (2 - old) * hb]

        def pop(half, nt):
            cols = pl.ds(nt * TILE, TILE)
            got = accv[half, :, cols]
            accv[half, :, cols] = jnp.zeros_like(got)
            return got

        def shard_rows(dev, q):
            return pl.ds(pl.multiple_of((dev * 4 + q) * ck, ck), ck)

        def sb_load(dev):
            return [
                pltpu.make_async_copy(a_hbm.at[shard_rows(dev, q)], sb.at[q], sb_sem.at[q])
                for q in range(4)
            ]

        def a_load(side, i):
            c = core if side == 0 else 1 - core
            dst = ad if side == 0 else ap
            if i < 4:
                src = [(2 * xl + c, i), (2 * xr + c, (i + 2) % 4)]
            else:
                src = [(2 * xf + c, i - 4), (2 * xf + c, i - 2)]
            return [
                pltpu.make_async_copy(a_hbm.at[shard_rows(dev, q)], dst.at[i, d], a_sem.at[side, i, d])
                for d, (dev, q) in enumerate(src)
            ]

        def a_wait(side, i):
            dst = ad if side == 0 else ap
            for d in range(2):
                pltpu.make_async_copy(
                    a_hbm.at[pl.ds(0, ck)], dst.at[i, d], a_sem.at[side, i, d]
                ).wait()

        def e_load(half, t):
            return pltpu.make_async_copy(e_hbm.at[t, half], eb.at[half], e_sem.at[half])

        def own_right(half, i):
            return remote(go.at[half, i], gd.at[half, i, 0], own_s.at[half, i, 0], d_r.at[half, i, 0], right)

        def own_left(half, i):
            q = (i + 2) % 4
            return remote(go.at[half, q], gd.at[half, i, 1], own_s.at[half, i, 1], d_r.at[half, i, 1], left)

        def own_partner(half):
            return remote(go.at[half], gl.at[half], pl_s.at[half], pl_r.at[half], partner)

        def fwd_right(half, i):
            return remote(gd.at[half, i, 0], gd.at[half, i + 4, 0], f_s.at[half, i, 0], d_r.at[half, i + 4, 0], right)

        def fwd_left(half, i):
            return remote(gd.at[half, i, 1], gd.at[half, i + 4, 1], f_s.at[half, i, 1], d_r.at[half, i + 4, 1], left)

        def fwd_partner(half, i):
            return remote(gd.at[half, i], gp.at[half, i], dp_s.at[half, i], dp_r.at[half, i], partner)

        def direct_wait(half, i):
            for d in range(2):
                remote(gd.at[half, i, d], gd.at[half, i, d], own_s.at[half, 0, d], d_r.at[half, i, d], right).wait_recv()

        def c_copy(half, j):
            return remote(cb.at[half, me], cb.at[half, me], c_s.at[half, j], c_r.at[half, me], (me + j) % n)

        def send_early(half):
            for i in range(3):
                own_right(half, i).start()
                own_left(half, i).start()
                if i == 0:
                    own_partner(half).start()

        def send_late(half):
            own_right(half, 3).start()
            own_left(half, 3).start()

        def direct(half, i, ring, first):
            direct_wait(half, i)

            def onward():
                fwd_right(half, i).start()
                fwd_left(half, i).start()

            if ring is not False:
                _when(ring, onward)
            fwd_partner(half, i).start()
            if first is not None:
                pl.when(first)(lambda: a_wait(0, i))

        def passed(half, i, first):
            fwd_partner(half, i).wait_recv()
            if first is not None:
                pl.when(first)(lambda: a_wait(1, i))

        def arrive(half, lo, hi, ring, first):
            def body(i, carry):
                direct(half, i, ring(i), first)
                passed(half, i - 1, first)
                mm(half, [(gd.at[half, i], ad.at[i]), (gp.at[half, i - 1], ap.at[i - 1])])
                return carry

            lax.fori_loop(lo, hi, body, 0)

        def sends_done(half):
            for i in range(4):
                own_right(half, i).wait_send()
                own_left(half, i).wait_send()
            own_partner(half).wait_send()
            for i in range(2):
                fwd_right(half, i).wait_send()
                fwd_left(half, i).wait_send()
            for i in range(SLOTS):
                fwd_partner(half, i).wait_send()

        def epilogue(half, t, start):
            e_load(half, 0).wait()
            part = jnp.zeros((hb, LANES), F32)
            for nt in range(ntiles):
                cols = pl.ds(nt * TILE, TILE)
                u = pop(half, nt)
                if start is not None:
                    pi_rows = jnp.broadcast_to(pi_ref[:, cols], (hb, TILE))
                    u = pi_rows if start is True else jnp.where(start, pi_rows, u)
                h = u * eb[half, :, cols].astype(F32)
                out_ref[half, :, cols] = h
                part = part + (h[:, :LANES] + h[:, LANES:])
            turned = jnp.concatenate([part] * (LANES // hb), axis=0).T
            cb[half, me] = jnp.sum(turned, axis=0, keepdims=True)
            pl.when(t + 1 < steps)(lambda: e_load(half, t + 1).start())
            for j in range(1, n):
                c_copy(half, j).start()

        def scale(half, t):
            for j in range(1, n):
                src = (me + j) % n
                remote(cb.at[half, src], cb.at[half, src], c_s.at[half, j], c_r.at[half, src], src).wait_recv()
                c_copy(half, j).wait_send()
            total = cb[half, 0]
            for j in range(1, n):
                total = total + cb[half, j]
            tot_ref[half, pl.ds(t, 1), :] = total
            inv = jnp.broadcast_to(k_total / total, (LANES, LANES)).T[:hb]
            for q in range(4):
                for s in range(ck // LANES):
                    cols = pl.ds(q * ck + s * LANES, LANES)
                    go[half, q, :, pl.ds(s * LANES, LANES)] = (out_ref[half, :, cols] * inv).astype(BF16)

            @pl.when(t == steps - 1)
            def _():
                for s in range(kl // LANES):
                    cols = pl.ds(s * LANES, LANES)
                    out_ref[half, :, cols] = out_ref[half, :, cols] * inv

        def phase(cur, old, k, live, have):
            start = None if have is True else jnp.logical_not(have)
            t = k + 1 if have is True else k
            _when(live, lambda: send_early(cur))
            old_first = k == 0 if old == 0 else None
            cur_first = k == 0 if cur == 0 else None
            last = SLOTS - 1

            def rest():
                arrive(old, 3, SLOTS, lambda i: False, old_first)
                passed(old, last, None)

            _when(have, rest)
            if cur == 0:
                pl.when(k == 0)(lambda: a_wait(1, last))
            else:
                own_partner(0).wait_recv()
                own_partner(1).wait_recv()
            for q in range(4):
                pltpu.make_async_copy(a_hbm.at[pl.ds(0, ck)], sb.at[q], sb_sem.at[q]).wait()
            mm_joint(old, gp.at[old, last], ap.at[last], go if cur == 0 else gl)

            def refill():
                for copy in sb_load(partner if cur == 0 else me):
                    copy.start()

            _when(live, refill)
            _when(have, lambda: sends_done(old))
            epilogue(old, t, start)

            def arrivals():
                send_late(cur)
                direct(cur, 0, True, cur_first)
                mm(cur, [(gd.at[cur, 0], ad.at[0])])
                arrive(cur, 1, 3, lambda i: i < 2, cur_first)

            _when(live, arrivals)
            scale(old, t)

        barrier = pltpu.get_barrier_semaphore()
        for j in range(1, n):
            pl.semaphore_signal(barrier, inc=1, device_id={"states": (me + j) % n}, device_id_type=MESH)
        accv[...] = jnp.zeros_like(accv)
        go[1] = jnp.zeros_like(go[1])
        gp[1, SLOTS - 1] = jnp.zeros_like(gp[1, SLOTS - 1])
        e_load(0, 0).start()
        e_load(1, 0).start()
        for c in sb_load(me):
            c.start()
        order = [(1, 5), (0, 0), (0, 1), (1, 0), (0, 2), (1, 1), (0, 3), (1, 2), (0, 4), (1, 3), (0, 5), (1, 4)]
        for side, i in order:
            for c in a_load(side, i):
                c.start()
        pl.semaphore_wait(barrier, n - 1)
        epilogue(0, 0, True)
        scale(0, 0)

        def step(k, carry):
            phase(0, 1, k, k < steps - 1, k >= 1)
            pl.when(k < steps - 1)(lambda: phase(1, 0, k, True, True))
            return carry

        lax.fori_loop(0, steps, step, 0)

    run()


def _forward(trans_mat, emit_steps, init_prob, n):
    k_total, kl = trans_mat.shape
    steps, _, hb, _ = emit_steps.shape
    ck = kl // 4
    dma = pltpu.SemaphoreType.DMA
    vmem = pl.BlockSpec(memory_space=pltpu.VMEM)
    hbm = pl.BlockSpec(memory_space=pl.ANY)
    return pl.pallas_call(
        functools.partial(_forward_kernel, (n, steps, hb, kl)),
        out_shape=(
            jax.ShapeDtypeStruct((2, steps, LANES), F32),
            jax.ShapeDtypeStruct((2, hb, kl), F32),
        ),
        in_specs=[hbm, hbm, vmem],
        out_specs=(vmem, vmem),
        scratch_shapes=[
            pltpu.VMEM((SLOTS, 2, ck, kl), BF16),
            pltpu.VMEM((SLOTS, 2, ck, kl), BF16),
            pltpu.VMEM((4, ck, kl), BF16),
            pltpu.VMEM((2, 4, hb, ck), BF16),
            pltpu.VMEM((2, 4, hb, ck), BF16),
            pltpu.VMEM((2, SLOTS, 2, hb, ck), BF16),
            pltpu.VMEM((2, SLOTS, 2, hb, ck), BF16),
            pltpu.VMEM((2, hb, kl), BF16),
            pltpu.VMEM((2, n, 1, LANES), F32),
            pltpu.VMEM((2, hb, kl), F32),
            dma((2, SLOTS, 2)),
            dma((4,)),
            dma((2,)),
            dma((2, 4, 2)),
            dma((2,)),
            dma((2,)),
            dma((2, SLOTS, 2)),
            dma((2, 2, 2)),
            dma((2, SLOTS)),
            dma((2, SLOTS)),
            dma((2, n)),
            dma((2, n)),
        ],
        compiler_params=pltpu.CompilerParams(
            collective_id=0, has_side_effects=True, vmem_limit_bytes=67043328
        ),
        name="hmm_forward",
    )(trans_mat, emit_steps, init_prob[None, :])


def solution(mesh):
    n = mesh.shape["states"]

    def local_forward(trans_mat, emit_mat, init_prob, tokens):
        vocab_size = emit_mat.shape[1]
        batch, steps = tokens.shape
        hb = batch // 2
        kl = trans_mat.shape[1]
        emit_steps = jnp.transpose(jnp.take(emit_mat, tokens.T, axis=1, mode="clip"), (1, 2, 0))
        totals, alpha = _forward(trans_mat, emit_steps.reshape(steps, 2, hb, kl), init_prob, n)
        norm = jnp.concatenate([totals[0, :, :hb], totals[1, :, :hb]], axis=1)
        first = jnp.arange(steps)[:, None] == 0
        norm = jnp.where(first, norm, norm / (n * kl))
        return jnp.log(norm * vocab_size).T, alpha.reshape(batch, kl)

    return jax.shard_map(
        local_forward,
        mesh=mesh,
        in_specs=(P(None, "states"), P("states", None), P("states"), P("seqs", None)),
        out_specs=(P("seqs", None), P("seqs", "states")),
        check_vma=False,
    )
```

time: 2260 us -> 865 us (0.38)
  waiting for transfers between devices: 917 us -> 0 us
  matrix products: 777 us -> 0 us
  Pallas kernels: 0 us -> 763 us
  blocking collectives: 389 us -> 0 us
  other arithmetic: 43.1 us -> 1.42 us
    all_gather x31 -> x0, waiting for transfers between devices: 916 us -> none  [advance(): lax.all_gather(alpha_prev.astype(jnp.bfloat16), 'states', axis=1, tiled=T...]
    dot_general x31 -> x0, matrix products: 777 us -> none  [advance(): mixed_u = jnp.dot(alpha_all, trans_mat, preferred_element_type=jnp.float32)]
    pallas_call x0 -> x1, Pallas kernels: none -> 763 us  [_forward(): pl.pallas_call(functools.partial(_forward_kernel, (n, steps, hb, kl)), ou...]
    psum x32 -> x0, blocking collectives: 389 us -> none  [the longest x31 375 us: advance(): norm_c = lax.psum(jnp.sum(raw_h, axis=-1), 'states') / k_total]
    convert_element_type x31 -> x0, other arithmetic: 26.6 us -> none  [advance(): alpha_prev.astype(jnp.bfloat16)]
  transfers between devices with their start and end apart: 31 -> 0, of which waited for: 31 -> 0; matrix products, arithmetic and copies ran while one was open for 0% -> 0% of each run, Pallas kernels for 0% -> 0%
where the time goes in v1:
time: 865 us; the launch traced here: 863 us
  Pallas kernels  763 us (88%)
  local copies, waits for them, and re-layouts  98.7 us (11%)
    pallas_call x1, Pallas kernels, _forward(): pl.pallas_call(functools.partial(_forward_kernel, (n, steps, hb, kl)), ou...  763 us
    gather x1, local copies, waits for them, and re-layouts, local_forward(): jnp.take(emit_mat, tokens.T, axis=1, mode='clip')  95.7 us

profile of v1, /device:TPU:113, one launch (start us, length us, event | category | flops | bytes accessed | tf_op | source)
XLA Modules:
  0.0 863.3 jit_solution(17471709942547136976)
XLA Ops:
  0.6 0.7 bitcast_clamp_fusion
  1.4 95.7 %gather_fusion = bf16[4096,2048]{1,0:T(8,128)(2,1)} fusion(bf16[2048,10000]{0,1:T(8,128)(2,1)} %param.5, s32[4096]{0:T(1024)S(1)} %bitcast_clamp_fusion), kind=kCustom, calls=%fused_computation | custom fusion | bytes 33570816 | tf_op jit(solution)/shard_map/jit(_take)/gather | solution.py:343
  97.0 762.5 %hmm_forward.1 = (f32[2,32,128]{2,1,0:T(8,128)}, f32[2,64,2048]{2,1,0:T(8,128)}) custom-call(bf16[16384,2048]{1,0:T(8,128)(2,1)} %a_hbm.1, bf16[32,2,64,2048]{3,2,1,0:T(8,128)(2,1)} %bitcast.13, f32[1,2048]{1,0:T(1,128)} %bitcast.15), custom_call_target="tpu_custom_call" | custom-call | tf_op jit(solution)/shard_map/hmm_forward/pallas_call | solution.py:296
  859.6 0.7 slice_bitcast_fusion.1
  860.3 0.7 fusion.2
  861.0 2.3 copy.7
  (1 shorter events, 0.0 us)

commit v2 on v1

--- a/solution.py
+++ b/solution.py
@@ -131,16 +131,12 @@
         def c_copy(half, j):
             return remote(cb.at[half, me], cb.at[half, me], c_s.at[half, j], c_r.at[half, me], (me + j) % n)
 
-        def send_early(half):
-            for i in range(3):
+        def send_own(half):
+            for i in range(4):
                 own_right(half, i).start()
                 own_left(half, i).start()
                 if i == 0:
                     own_partner(half).start()
-
-        def send_late(half):
-            own_right(half, 3).start()
-            own_left(half, 3).start()
 
         def direct(half, i, ring, first):
             direct_wait(half, i)
@@ -160,9 +156,10 @@
             if first is not None:
                 pl.when(first)(lambda: a_wait(1, i))
 
-        def arrive(half, lo, hi, ring, first):
+        def arrive(half, lo, hi, ring, first, also=lambda i: None):
             def body(i, carry):
                 direct(half, i, ring(i), first)
+                also(i)
                 passed(half, i - 1, first)
                 mm(half, [(gd.at[half, i], ad.at[i]), (gp.at[half, i - 1], ap.at[i - 1])])
                 return carry
@@ -194,9 +191,9 @@
                 part = part + (h[:, :LANES] + h[:, LANES:])
             turned = jnp.concatenate([part] * (LANES // hb), axis=0).T
             cb[half, me] = jnp.sum(turned, axis=0, keepdims=True)
-            pl.when(t + 1 < steps)(lambda: e_load(half, t + 1).start())
             for j in range(1, n):
                 c_copy(half, j).start()
+            pl.when(t + 1 < steps)(lambda: e_load(half, t + 1).start())
 
         def scale(half, t):
             for j in range(1, n):
@@ -222,7 +219,7 @@
         def phase(cur, old, k, live, have):
             start = None if have is True else jnp.logical_not(have)
             t = k + 1 if have is True else k
-            _when(live, lambda: send_early(cur))
+            _when(live, lambda: send_own(cur))
             old_first = k == 0 if old == 0 else None
             cur_first = k == 0 if cur == 0 else None
             last = SLOTS - 1
@@ -241,19 +238,22 @@
                 pltpu.make_async_copy(a_hbm.at[pl.ds(0, ck)], sb.at[q], sb_sem.at[q]).wait()
             mm_joint(old, gp.at[old, last], ap.at[last], go if cur == 0 else gl)
 
-            def refill():
-                for copy in sb_load(partner if cur == 0 else me):
-                    copy.start()
-
-            _when(live, refill)
+            def refill(i):
+                copies = sb_load(partner if cur == 0 else me)
+                for part in range(2):
+
+                    @pl.when(i == part + 1)
+                    def _():
+                        copies[2 * part].start()
+                        copies[2 * part + 1].start()
+
             _when(have, lambda: sends_done(old))
             epilogue(old, t, start)
 
             def arrivals():
-                send_late(cur)
                 direct(cur, 0, True, cur_first)
                 mm(cur, [(gd.at[cur, 0], ad.at[0])])
-                arrive(cur, 1, 3, lambda i: i < 2, cur_first)
+                arrive(cur, 1, 3, lambda i: i < 2, cur_first, refill)
 
             _when(live, arrivals)
             scale(old, t)

time: 865 us -> 865 us (level)
  no operation moved by 1% of the time
where the time goes in v2:
time: 865 us; the launch traced here: 863 us
  Pallas kernels  762 us (88%)
  local copies, waits for them, and re-layouts  98.7 us (11%)
    pallas_call x1, Pallas kernels, _forward(): pl.pallas_call(functools.partial(_forward_kernel, (n, steps, hb, kl)), ou...  762 us
    gather x1, local copies, waits for them, and re-layouts, local_forward(): jnp.take(emit_mat, tokens.T, axis=1, mode='clip')  95.7 us

profile of v2, /device:TPU:113, one launch (start us, length us, event | category | flops | bytes accessed | tf_op | source)
XLA Modules:
  0.0 862.9 jit_solution(13380989241586052682)
XLA Ops:
  0.6 0.7 bitcast_clamp_fusion
  1.4 95.7 %gather_fusion = bf16[4096,2048]{1,0:T(8,128)(2,1)} fusion(bf16[2048,10000]{0,1:T(8,128)(2,1)} %param.5, s32[4096]{0:T(1024)S(1)} %bitcast_clamp_fusion), kind=kCustom, calls=%fused_computation | custom fusion | bytes 33570816 | tf_op jit(solution)/shard_map/jit(_take)/gather | solution.py:343
  97.0 762.1 %hmm_forward.1 = (f32[2,32,128]{2,1,0:T(8,128)}, f32[2,64,2048]{2,1,0:T(8,128)}) custom-call(bf16[16384,2048]{1,0:T(8,128)(2,1)} %a_hbm.1, bf16[32,2,64,2048]{3,2,1,0:T(8,128)(2,1)} %bitcast.13, f32[1,2048]{1,0:T(1,128)} %bitcast.15), custom_call_target="tpu_custom_call" | custom-call | tf_op jit(solution)/shard_map/hmm_forward/pallas_call | solution.py:296
  859.2 0.7 slice_bitcast_fusion.1
  859.9 0.7 fusion.2
  860.6 2.3 copy.7
  (1 shorter events, 0.0 us)

commit v3 on v2

--- a/solution.py
+++ b/solution.py
@@ -11,6 +11,7 @@
 F32 = jnp.float32
 BF16 = jnp.bfloat16
 LANES = 128
+BUFS = 4
 SLOTS = 6
 TILE = 256
 
@@ -24,7 +25,7 @@
 
 def _forward_kernel(
     dims, a_hbm, e_hbm, pi_ref, tot_ref, out_ref,
-    ad, ap, sb, go, gl, gd, gp, eb, cb, accv,
+    ad, ap, sb, go, gd, gp, eb, cb, accv,
     a_sem, sb_sem, e_sem, own_s, pl_s, pl_r, d_r, f_s, dp_s, dp_r, c_s, c_r,
 ):
     n, steps, hb, kl = dims
@@ -55,18 +56,18 @@
                         total += jnp.dot(lhs[q], rhs[q, :, cols], preferred_element_type=F32)
                 accv[half, :, cols] = total
 
-        def mm_joint(old, lhs, rhs, shared):
+        def mm_joint(cur, old, lhs, rhs, shared):
             for nt in range(ntiles):
                 cols = pl.ds(nt * TILE, TILE)
-                both = jnp.concatenate([accv[0, :, cols], accv[1, :, cols]], axis=0)
+                both = jnp.concatenate([accv[cur, :, cols], accv[old, :, cols]], axis=0)
                 for q in range(4):
-                    rows = jnp.concatenate([shared[0, q], shared[1, q]], axis=0)
+                    rows = jnp.concatenate([shared[cur, q], shared[old, q]], axis=0)
                     both += jnp.dot(rows, sb[q, :, cols], preferred_element_type=F32)
-                own = both[old * hb : (old + 1) * hb]
+                own = both[hb:]
                 for q in range(rhs.shape[0]):
                     own += jnp.dot(lhs[q], rhs[q, :, cols], preferred_element_type=F32)
                 accv[old, :, cols] = own
-                accv[1 - old, :, cols] = both[(1 - old) * hb : (2 - old) * hb]
+                accv[cur, :, cols] = both[:hb]
 
         def pop(half, nt):
             cols = pl.ds(nt * TILE, TILE)
@@ -106,14 +107,14 @@
             return pltpu.make_async_copy(e_hbm.at[t, half], eb.at[half], e_sem.at[half])
 
         def own_right(half, i):
-            return remote(go.at[half, i], gd.at[half, i, 0], own_s.at[half, i, 0], d_r.at[half, i, 0], right)
+            return remote(go.at[0, half, i], gd.at[half, i, 0], own_s.at[half, i, 0], d_r.at[half, i, 0], right)
 
         def own_left(half, i):
             q = (i + 2) % 4
-            return remote(go.at[half, q], gd.at[half, i, 1], own_s.at[half, i, 1], d_r.at[half, i, 1], left)
+            return remote(go.at[0, half, q], gd.at[half, i, 1], own_s.at[half, i, 1], d_r.at[half, i, 1], left)
 
         def own_partner(half):
-            return remote(go.at[half], gl.at[half], pl_s.at[half], pl_r.at[half], partner)
+            return remote(go.at[0, half], go.at[1, half], pl_s.at[half], pl_r.at[half], partner)
 
         def fwd_right(half, i):
             return remote(gd.at[half, i, 0], gd.at[half, i + 4, 0], f_s.at[half, i, 0], d_r.at[half, i + 4, 0], right)
@@ -208,7 +209,7 @@
             for q in range(4):
                 for s in range(ck // LANES):
                     cols = pl.ds(q * ck + s * LANES, LANES)
-                    go[half, q, :, pl.ds(s * LANES, LANES)] = (out_ref[half, :, cols] * inv).astype(BF16)
+                    go[0, half, q, :, pl.ds(s * LANES, LANES)] = (out_ref[half, :, cols] * inv).astype(BF16)
 
             @pl.when(t == steps - 1)
             def _():
@@ -216,30 +217,36 @@
                     cols = pl.ds(s * LANES, LANES)
                     out_ref[half, :, cols] = out_ref[half, :, cols] * inv
 
-        def phase(cur, old, k, live, have):
-            start = None if have is True else jnp.logical_not(have)
-            t = k + 1 if have is True else k
-            _when(live, lambda: send_own(cur))
-            old_first = k == 0 if old == 0 else None
-            cur_first = k == 0 if cur == 0 else None
+        def phase(p, carry):
+            cur = lax.rem(p, 2)
+            old = 1 - cur
+            t = lax.div(p + 1, 2)
             last = SLOTS - 1
-
-            def rest():
-                arrive(old, 3, SLOTS, lambda i: False, old_first)
+            live = p < 2 * steps - 2
+            have = p >= 1
+            pl.when(live)(lambda: send_own(cur))
+
+            @pl.when(have)
+            def _():
+                arrive(old, 3, SLOTS, lambda i: False, p == 1)
                 passed(old, last, None)
 
-            _when(have, rest)
-            if cur == 0:
-                pl.when(k == 0)(lambda: a_wait(1, last))
-            else:
+            pl.when(p == 0)(lambda: a_wait(1, last))
+
+            @pl.when(cur == 1)
+            def _():
                 own_partner(0).wait_recv()
                 own_partner(1).wait_recv()
+
             for q in range(4):
                 pltpu.make_async_copy(a_hbm.at[pl.ds(0, ck)], sb.at[q], sb_sem.at[q]).wait()
-            mm_joint(old, gp.at[old, last], ap.at[last], go if cur == 0 else gl)
+            mm_joint(cur, old, gp.at[old, last], ap.at[last], go.at[cur])
+            pl.when(have)(lambda: sends_done(old))
+            epilogue(old, t, p == 0)
+            following = partner * (1 - cur) + me * cur
 
             def refill(i):
-                copies = sb_load(partner if cur == 0 else me)
+                copies = sb_load(following)
                 for part in range(2):
 
                     @pl.when(i == part + 1)
@@ -247,22 +254,20 @@
                         copies[2 * part].start()
                         copies[2 * part + 1].start()
 
-            _when(have, lambda: sends_done(old))
-            epilogue(old, t, start)
-
-            def arrivals():
-                direct(cur, 0, True, cur_first)
+            @pl.when(live)
+            def _():
+                direct(cur, 0, True, p == 0)
                 mm(cur, [(gd.at[cur, 0], ad.at[0])])
-                arrive(cur, 1, 3, lambda i: i < 2, cur_first, refill)
-
-            _when(live, arrivals)
+                arrive(cur, 1, 3, lambda i: i < 2, p == 0, refill)
+
             scale(old, t)
+            return carry
 
         barrier = pltpu.get_barrier_semaphore()
         for j in range(1, n):
             pl.semaphore_signal(barrier, inc=1, device_id={"states": (me + j) % n}, device_id_type=MESH)
         accv[...] = jnp.zeros_like(accv)
-        go[1] = jnp.zeros_like(go[1])
+        go[0, 1] = jnp.zeros_like(go[0, 1])
         gp[1, SLOTS - 1] = jnp.zeros_like(gp[1, SLOTS - 1])
         e_load(0, 0).start()
         e_load(1, 0).start()
@@ -276,12 +281,7 @@
         epilogue(0, 0, True)
         scale(0, 0)
 
-        def step(k, carry):
-            phase(0, 1, k, k < steps - 1, k >= 1)
-            pl.when(k < steps - 1)(lambda: phase(1, 0, k, True, True))
-            return carry
-
-        lax.fori_loop(0, steps, step, 0)
+        lax.fori_loop(0, 2 * steps - 1, phase, 0)
 
     run()
 
@@ -305,8 +305,7 @@
             pltpu.VMEM((SLOTS, 2, ck, kl), BF16),
             pltpu.VMEM((SLOTS, 2, ck, kl), BF16),
             pltpu.VMEM((4, ck, kl), BF16),
-            pltpu.VMEM((2, 4, hb, ck), BF16),
-            pltpu.VMEM((2, 4, hb, ck), BF16),
+            pltpu.VMEM((2, 2, 4, hb, ck), BF16),
             pltpu.VMEM((2, SLOTS, 2, hb, ck), BF16),
             pltpu.VMEM((2, SLOTS, 2, hb, ck), BF16),
             pltpu.VMEM((2, hb, kl), BF16),
@@ -332,6 +331,53 @@
     )(trans_mat, emit_steps, init_prob[None, :])
 
 
+def _gather_kernel(tok_ref, sub_ref, em_hbm, out_ref, buf, sem):
+    g, groups = pl.program_id(0), pl.num_programs(0)
+    hb = out_ref.shape[0]
+
+    def fetch(group, slot):
+        for b in range(hb):
+            row = lax.shift_left(lax.shift_right_logical(tok_ref[group * hb + b], 3), 3)
+            pltpu.make_async_copy(
+                em_hbm.at[pl.ds(pl.multiple_of(row, 8), 8)], buf.at[slot, pl.ds(b * 8, 8)], sem.at[slot]
+            ).start(priority=b % 2)
+
+    slot = lax.rem(g, BUFS)
+
+    @pl.when(g == 0)
+    def _():
+        for ahead in range(BUFS - 1):
+            fetch(ahead, ahead)
+
+    @pl.when(g + BUFS - 1 < groups)
+    def _():
+        fetch(g + BUFS - 1, lax.rem(g + BUFS - 1, BUFS))
+
+    pltpu.make_async_copy(em_hbm.at[pl.ds(0, hb * 8)], buf.at[slot], sem.at[slot]).wait()
+    col = lax.broadcasted_iota(jnp.int32, (hb, hb * 8), 1)
+    row = lax.broadcasted_iota(jnp.int32, (hb, hb * 8), 0)
+    pick = (col == row * 8 + sub_ref[...]).astype(F32).astype(BF16)
+    out_ref[...] = jnp.dot(pick, buf[slot], preferred_element_type=F32).astype(BF16)
+
+
+def _gather_rows(table, tokens, hb):
+    kl = table.shape[1]
+    count = tokens.shape[0]
+    return pl.pallas_call(
+        _gather_kernel,
+        grid_spec=pltpu.PrefetchScalarGridSpec(
+            num_scalar_prefetch=1,
+            grid=(count // hb,),
+            in_specs=[pl.BlockSpec((hb, 1), lambda g, t: (g, 0)), pl.BlockSpec(memory_space=pl.ANY)],
+            out_specs=pl.BlockSpec((hb, kl), lambda g, t: (g, 0)),
+            scratch_shapes=[pltpu.VMEM((BUFS, hb * 8, kl), BF16), pltpu.SemaphoreType.DMA((BUFS,))],
+        ),
+        out_shape=jax.ShapeDtypeStruct((count, kl), BF16),
+        compiler_params=pltpu.CompilerParams(vmem_limit_bytes=67043328),
+        name="emit_gather",
+    )(tokens, lax.bitwise_and(tokens, 7)[:, None], table)
+
+
 def solution(mesh):
     n = mesh.shape["states"]
 
@@ -340,7 +386,7 @@
         batch, steps = tokens.shape
         hb = batch // 2
         kl = trans_mat.shape[1]
-        emit_steps = jnp.transpose(jnp.take(emit_mat, tokens.T, axis=1, mode="clip"), (1, 2, 0))
+        emit_steps = _gather_rows(emit_mat.T, tokens.T.reshape(-1), hb)
         totals, alpha = _forward(trans_mat, emit_steps.reshape(steps, 2, hb, kl), init_prob, n)
         norm = jnp.concatenate([totals[0, :, :hb], totals[1, :, :hb]], axis=1)
         first = jnp.arange(steps)[:, None] == 0

time: 865 us -> 840 us (0.971)
  local copies, waits for them, and re-layouts: 98.7 us -> 5.03 us
  Pallas kernels: 762 us -> 829 us
    gather x1 -> x0, local copies, waits for them, and re-layouts: 95.7 us -> none  [local_forward(): jnp.take(emit_mat, tokens.T, axis=1, mode='clip')]
    pallas_call x0 -> x1, Pallas kernels: none -> 54.6 us  [_gather_rows(): pl.pallas_call(_gather_kernel, grid_spec=pltpu.PrefetchScalarGridSpec(num...]
    pallas_call x1, Pallas kernels: 762 us -> 775 us  [_forward(): pl.pallas_call(functools.partial(_forward_kernel, (n, steps, hb, kl)), ou...]
where the time goes in v3:
time: 840 us; the launch traced here: 836 us
  Pallas kernels  829 us (99%)
    pallas_call x1, Pallas kernels, _forward(): pl.pallas_call(functools.partial(_forward_kernel, (n, steps, hb, kl)), ou...  775 us
    pallas_call x1, Pallas kernels, _gather_rows(): pl.pallas_call(_gather_kernel, grid_spec=pltpu.PrefetchScalarGridSpec(num...  54.6 us

profile of v3, /device:TPU:113, one launch (start us, length us, event | category | flops | bytes accessed | tf_op | source)
XLA Modules:
  0.0 836.4 jit_solution(7275352294245918235)
XLA Ops:
  0.6 0.7 bitcast_and_fusion
  1.4 2.0 copy.6.sub_ref
  3.3 54.6 %emit_gather.1 = bf16[4096,2048]{1,0:T(8,128)(2,1)} custom-call(s32[4096]{0:T(1024)} %bitcast.18, s32[4096,1]{1,0:T(8,128)} %copy.6.sub_ref, bf16[10000,2048]{1,0:T(8,128)(2,1)} %bitcast.16), custom_call_target="tpu_custom_call" | custom-call | tf_op jit(solution)/shard_map/emit_gather/pallas_call | solution.py:366
  58.0 774.7 %hmm_forward.1 = (f32[2,32,128]{2,1,0:T(8,128)}, f32[2,64,2048]{2,1,0:T(8,128)}) custom-call(bf16[16384,2048]{1,0:T(8,128)(2,1)} %a_hbm.1, bf16[32,2,64,2048]{3,2,1,0:T(8,128)(2,1)} %bitcast.15, f32[1,2048]{1,0:T(1,128)} %bitcast.20), custom_call_target="tpu_custom_call" | custom-call | tf_op jit(solution)/shard_map/hmm_forward/pallas_call | solution.py:296
  832.7 0.7 slice_bitcast_fusion.1
  833.4 0.7 fusion.2
  834.1 2.3 copy.8
  (1 shorter events, 0.0 us)

commit v4 on v2

--- a/solution.py
+++ b/solution.py
@@ -11,6 +11,7 @@
 F32 = jnp.float32
 BF16 = jnp.bfloat16
 LANES = 128
+BUFS = 4
 SLOTS = 6
 TILE = 256
 
@@ -332,6 +333,53 @@
     )(trans_mat, emit_steps, init_prob[None, :])
 
 
+def _gather_kernel(tok_ref, sub_ref, em_hbm, out_ref, buf, sem):
+    g, groups = pl.program_id(0), pl.num_programs(0)
+    hb = out_ref.shape[0]
+
+    def fetch(group, slot):
+        for b in range(hb):
+            row = lax.shift_left(lax.shift_right_logical(tok_ref[group * hb + b], 3), 3)
+            pltpu.make_async_copy(
+                em_hbm.at[pl.ds(pl.multiple_of(row, 8), 8)], buf.at[slot, pl.ds(b * 8, 8)], sem.at[slot]
+            ).start(priority=b % 2)
+
+    slot = lax.rem(g, BUFS)
+
+    @pl.when(g == 0)
+    def _():
+        for ahead in range(BUFS - 1):
+            fetch(ahead, ahead)
+
+    @pl.when(g + BUFS - 1 < groups)
+    def _():
+        fetch(g + BUFS - 1, lax.rem(g + BUFS - 1, BUFS))
+
+    pltpu.make_async_copy(em_hbm.at[pl.ds(0, hb * 8)], buf.at[slot], sem.at[slot]).wait()
+    col = lax.broadcasted_iota(jnp.int32, (hb, hb * 8), 1)
+    row = lax.broadcasted_iota(jnp.int32, (hb, hb * 8), 0)
+    pick = (col == row * 8 + sub_ref[...]).astype(F32).astype(BF16)
+    out_ref[...] = jnp.dot(pick, buf[slot], preferred_element_type=F32).astype(BF16)
+
+
+def _gather_rows(table, tokens, hb):
+    kl = table.shape[1]
+    count = tokens.shape[0]
+    return pl.pallas_call(
+        _gather_kernel,
+        grid_spec=pltpu.PrefetchScalarGridSpec(
+            num_scalar_prefetch=1,
+            grid=(count // hb,),
+            in_specs=[pl.BlockSpec((hb, 1), lambda g, t: (g, 0)), pl.BlockSpec(memory_space=pl.ANY)],
+            out_specs=pl.BlockSpec((hb, kl), lambda g, t: (g, 0)),
+            scratch_shapes=[pltpu.VMEM((BUFS, hb * 8, kl), BF16), pltpu.SemaphoreType.DMA((BUFS,))],
+        ),
+        out_shape=jax.ShapeDtypeStruct((count, kl), BF16),
+        compiler_params=pltpu.CompilerParams(vmem_limit_bytes=67043328),
+        name="emit_gather",
+    )(tokens, lax.bitwise_and(tokens, 7)[:, None], table)
+
+
 def solution(mesh):
     n = mesh.shape["states"]
 
@@ -340,7 +388,7 @@
         batch, steps = tokens.shape
         hb = batch // 2
         kl = trans_mat.shape[1]
-        emit_steps = jnp.transpose(jnp.take(emit_mat, tokens.T, axis=1, mode="clip"), (1, 2, 0))
+        emit_steps = _gather_rows(emit_mat.T, tokens.T.reshape(-1), hb)
         totals, alpha = _forward(trans_mat, emit_steps.reshape(steps, 2, hb, kl), init_prob, n)
         norm = jnp.concatenate([totals[0, :, :hb], totals[1, :, :hb]], axis=1)
         first = jnp.arange(steps)[:, None] == 0

time: 865 us -> 827 us (0.956)
  local copies, waits for them, and re-layouts: 98.7 us -> 5.03 us
  Pallas kernels: 762 us -> 817 us
    gather x1 -> x0, local copies, waits for them, and re-layouts: 95.7 us -> none  [local_forward(): jnp.take(emit_mat, tokens.T, axis=1, mode='clip')]
    pallas_call x0 -> x1, Pallas kernels: none -> 54.5 us  [_gather_rows(): pl.pallas_call(_gather_kernel, grid_spec=pltpu.PrefetchScalarGridSpec(num...]
where the time goes in v4:
time: 827 us; the launch traced here: 824 us
  Pallas kernels  817 us (99%)
    pallas_call x1, Pallas kernels, _forward(): pl.pallas_call(functools.partial(_forward_kernel, (n, steps, hb, kl)), ou...  762 us
    pallas_call x1, Pallas kernels, _gather_rows(): pl.pallas_call(_gather_kernel, grid_spec=pltpu.PrefetchScalarGridSpec(num...  54.5 us

profile of v4, /device:TPU:113, one launch (start us, length us, event | category | flops | bytes accessed | tf_op | source)
XLA Modules:
  0.0 823.8 jit_solution(15317131768945835461)
XLA Ops:
  0.6 0.7 bitcast_and_fusion
  1.4 2.0 copy.6.sub_ref
  3.3 54.5 %emit_gather.1 = bf16[4096,2048]{1,0:T(8,128)(2,1)} custom-call(s32[4096]{0:T(1024)} %bitcast.18, s32[4096,1]{1,0:T(8,128)} %copy.6.sub_ref, bf16[10000,2048]{1,0:T(8,128)(2,1)} %bitcast.16), custom_call_target="tpu_custom_call" | custom-call | tf_op jit(solution)/shard_map/emit_gather/pallas_call | solution.py:368
  57.9 762.1 %hmm_forward.1 = (f32[2,32,128]{2,1,0:T(8,128)}, f32[2,64,2048]{2,1,0:T(8,128)}) custom-call(bf16[16384,2048]{1,0:T(8,128)(2,1)} %a_hbm.1, bf16[32,2,64,2048]{3,2,1,0:T(8,128)(2,1)} %bitcast.15, f32[1,2048]{1,0:T(1,128)} %bitcast.20), custom_call_target="tpu_custom_call" | custom-call | tf_op jit(solution)/shard_map/hmm_forward/pallas_call | solution.py:297
  820.0 0.7 slice_bitcast_fusion.1
  820.8 0.7 fusion.2
  821.5 2.3 copy.8
  (1 shorter events, 0.0 us)
